TPU v7x, 32 devices: a whole 2x2x4 slice. The times are simulated.
32 devices in a mesh: group: 2 (over x), ep: 16 (over z, y, core).
Axes of the slice: x: 2, y: 2, z: 4, core: 2. Of those that a mesh axis runs over, the one named last changes fastest.
Arguments:
- tokens: bfloat16 [2048, 3072], P(('group', 'ep')), parts along dimension 0, may hold values from -6 to 6
- expert_ids: int32 [2048, 2], P(('group', 'ep')), parts along dimension 0, may hold values from 0 to 3, all different within a row; in each aligned block of 64 rows (0 to 63, 64 to 127, ...) at most 48 rows name the same one
- w_router: bfloat16 [3072, 4], replicated, may hold values from -0.109375 to 0.109375
- w_gate: bfloat16 [3072, 32768], P(None, 'ep'), may hold values from -0.109375 to 0.109375
- w_up: bfloat16 [3072, 32768], P(None, 'ep'), may hold values from -0.109375 to 0.109375
- w_down: bfloat16 [32768, 3072], P('ep'), may hold values from -0.0625 to 0.0625
- queries: bfloat16 [256, 24, 128], P(('group', 'ep')), parts along dimension 0, may hold values from -48 to 48
- key_cache: bfloat16 [256, 256, 4, 128], P(('group', 'ep')), parts along dimension 0, may hold values from -48 to 48
- cached_value_rows: bfloat16 [256, 256, 4, 128], P(('group', 'ep')), parts along dimension 0, may hold values from -6 to 6
- lengths: int32 [256], P(('group', 'ep')), parts along dimension 0, may hold values from 2 to 256, as said below
Outputs:
- moe_out: bfloat16 [2048, 3072], P(('group', 'ep')), parts along dimension 0
- attention_out: bfloat16 [256, 24, 128], P(('group', 'ep')), parts along dimension 0
There are 2 independent parts, one for each index of `group`. A program takes and returns all parts, laid end to end along the dimension named above; an argument that names none is the same for every part. Nothing has to cross between parts.
Inputs may be any that keep to these rules, and one draw needn't show every extreme that they name: `expert_ids`: each row names two different experts; among the rows of one device no expert is named more than 48 times, and some device has an expert named exactly 48 times. `lengths`: every device holds a request of length 256.
All inputs are finite; a program needn't handle non-finite values.
Results may differ from a plain program's by a relative error of at most 0.0085.
Values may be sent and summed in bfloat16 or wider, within the bound.
A program may use at most 128 MiB of HBM per device.

v0:
```python
import functools

import jax
import jax.numpy as jnp
from jax import lax
from jax.experimental import pallas as pl
from jax.experimental.pallas import tpu as pltpu
from jax.sharding import PartitionSpec as P

CAP = 48
ORDER = (0, 2, 3, 1)
UP_TILE = 512
DOWN_TILE = 1024
VMEM_LIMIT = 66_000_000


def flip(index, mask):
    result = index
    bit = 1
    while bit <= mask:
        if mask & bit:
            result = result + bit - 2 * bit * ((index // bit) % 2)
        bit *= 2
    return result


def moe_kernel(
    plane,
    kv_heads,
    packed,
    comb_hi,
    comb_lo,
    queries,
    lengths,
    wg_hbm,
    wu_hbm,
    wd_hbm,
    k_hbm,
    v_hbm,
    out,
    att_out,
    wg,
    wu,
    wd,
    keys,
    values,
    arrived,
    hidden,
    partial,
    got_core,
    got_y,
    got_z,
    w_sems,
    d_sems,
    kv_sems,
    own_sem,
    send_sems,
    recv_sems,
):
    me = lax.axis_index("ep")
    experts = packed.shape[0]
    features = packed.shape[2]
    core_peer = flip(me, 1)
    y_peer = flip(me, 2)
    z_peers = [flip(me, plane * d) for d in range(experts)]
    n_up = wg.shape[0]
    n_down = wd.shape[0]
    up_tile = wg.shape[2]
    down_tile = wd.shape[2]

    def kv_copy(i):
        src, dst = ((k_hbm, keys), (v_hbm, values))[i]
        return pltpu.make_async_copy(src, dst, kv_sems.at[i])

    def up_copy(i, j):
        src, dst = ((wg_hbm, wg), (wu_hbm, wu))[i]
        cols = pl.ds(pl.multiple_of(j * up_tile, up_tile), up_tile)
        return pltpu.make_async_copy(src.at[:, cols], dst.at[j], w_sems.at[i, j])

    def down_copy(j):
        cols = pl.ds(pl.multiple_of(j * down_tile, down_tile), down_tile)
        return pltpu.make_async_copy(wd_hbm.at[:, cols], wd.at[j], d_sems.at[j])

    barrier = pltpu.get_barrier_semaphore()
    peers = [core_peer, y_peer] + z_peers[1:]
    for peer in peers:
        pl.semaphore_signal(
            barrier, inc=1, device_id={"ep": peer}, device_id_type=pl.DeviceIdType.MESH
        )
    own = pltpu.make_async_copy(packed.at[0], arrived.at[0, 0], own_sem)
    own.start()
    kv_copy(0).start()
    kv_copy(1).start()
    pl.semaphore_wait(barrier, len(peers))

    def remote(kind, d, src, dst, peer):
        return pltpu.make_async_remote_copy(
            src_ref=src,
            dst_ref=dst,
            send_sem=send_sems.at[kind, d],
            recv_sem=recv_sems.at[kind, d],
            device_id={"ep": peer},
            device_id_type=pl.DeviceIdType.MESH,
        )

    def first(d):
        return packed.at[0] if d == 0 else arrived.at[d, 0]

    z_out = [
        remote(0, d, packed.at[d], arrived.at[d, 0], z_peers[d]) if d else None
        for d in range(experts)
    ]
    y_out = [remote(1, d, first(d), arrived.at[d, 1], y_peer) for d in range(experts)]
    c_out = [remote(2, d, first(d), arrived.at[d, 2], core_peer) for d in range(experts)]
    f_out = [
        remote(3, d, arrived.at[d, 1], arrived.at[d, 3], core_peer) for d in range(experts)
    ]
    def c_back(d, j):
        return remote(
            4, d * n_down + j, partial.at[d, j, pl.ds(2, 2)], got_core.at[d, j], core_peer
        )

    def y_back(d, j):
        return remote(5, d * n_down + j, partial.at[d, j, 1], got_y.at[d, j], y_peer)

    def z_back(d, j):
        return remote(6, d * n_down + j, partial.at[d, j, 0], got_z.at[d, j], z_peers[d])

    def spread(d):
        if d > 0:
            z_out[d].wait_recv()
        y_out[d].start()
        c_out[d].start()

    def forward(d):
        y_out[d].wait_recv()
        f_out[d].start()

    def settle(d):
        c_out[d].wait_recv()
        f_out[d].wait_recv()

    for d in ORDER:
        if d > 0:
            z_out[d].start()
    spread(0)
    for j in range(n_up):
        up_copy(0, j).start()
        up_copy(1, j).start()
    for j in range(n_down):
        down_copy(j).start()

    kv_copy(0).wait()
    kv_copy(1).wait()
    heads, head_dim = queries.shape[1], queries.shape[2]
    rows = keys.shape[1]

    def attend(r, carry):
        scores = lax.dot_general(
            queries[r], keys[r], (((1,), (1,)), ((), ())), preferred_element_type=jnp.float32
        ) * head_dim ** (-0.5)
        col = lax.broadcasted_iota(jnp.int32, (heads, rows), 1)
        head = lax.broadcasted_iota(jnp.int32, (heads, rows), 0)
        keep = (col % kv_heads == head // (heads // kv_heads)) & (
            col // kv_heads < lengths[r]
        )
        scores = jnp.where(keep, scores, -jnp.inf)
        top = jnp.max(scores, axis=1, keepdims=True)
        expo = jnp.exp(scores - top)
        weights = (expo / jnp.sum(expo, axis=1, keepdims=True)).astype(jnp.bfloat16)
        mixed = jnp.dot(weights, values[r], preferred_element_type=jnp.float32)
        att_out[r] = mixed.astype(att_out.dtype)
        return carry

    lax.fori_loop(0, queries.shape[0], attend, 0)

    def gate_up(d, wait):
        block = arrived.at[d]
        m = block.shape[0] * block.shape[1]

        def step(j, carry):
            if wait:
                up_copy(0, j).wait()
                up_copy(1, j).wait()
            x = block[...].reshape(m, features)
            g = jnp.dot(x, wg[j], preferred_element_type=jnp.float32)
            u = jnp.dot(x, wu[j], preferred_element_type=jnp.float32)
            hidden[j] = (g / (1.0 + jnp.exp(-g)) * u).astype(jnp.bfloat16)
            return carry

        lax.fori_loop(0, n_up, step, 0)

    def down(d, wait):
        m = hidden.shape[1]

        def step(j, carry):
            if wait:
                down_copy(j).wait()
            h = jnp.concatenate([hidden[i] for i in range(n_up)], axis=1)
            o = jnp.dot(h, wd[j], preferred_element_type=jnp.float32)
            partial[d, j] = o.astype(jnp.bfloat16).reshape(partial.shape[2:])
            c_back(d, j).start()
            return carry

        lax.fori_loop(0, n_down, step, 0)

    def sum_core(d):
        def step(j, carry):
            c_back(d, j).wait_recv()
            for s in (1, 0):
                partial[d, j, s] = (
                    partial[d, j, s].astype(jnp.float32) + got_core[d, j, s].astype(jnp.float32)
                ).astype(jnp.bfloat16)
            y_back(d, j).start()
            return carry

        lax.fori_loop(0, n_down, step, 0)

    def sum_y(d):
        def step(j, carry):
            y_back(d, j).wait_recv()
            total = partial[d, j, 0].astype(jnp.float32) + got_y[d, j].astype(jnp.float32)
            if d == 0:
                got_z[0, j] = total.astype(jnp.bfloat16)
            else:
                partial[d, j, 0] = total.astype(jnp.bfloat16)
                z_back(d, j).start()
            return carry

        lax.fori_loop(0, n_down, step, 0)

    own.wait()
    forward(ORDER[0])
    spread(ORDER[1])
    settle(ORDER[0])
    for i, d in enumerate(ORDER):
        last = i + 1 == experts
        if i > 0:
            settle(d)
        gate_up(d, i == 0)
        if not last:
            forward(ORDER[i + 1])
        if i > 0:
            sum_core(ORDER[i - 1])
        if i + 2 < experts:
            spread(ORDER[i + 2])
        down(d, i == 0)
        if i > 0:
            sum_y(ORDER[i - 1])
    sum_core(ORDER[-1])
    sum_y(ORDER[-1])
    for j in range(n_down):
        for d in range(1, experts):
            z_back(d, j).wait_recv()
        returned = got_z[:, j].reshape(experts * got_z.shape[2], down_tile)
        out[:, j * down_tile : (j + 1) * down_tile] = (
            jnp.dot(comb_hi[...], returned, preferred_element_type=jnp.float32)
            + jnp.dot(comb_lo[...], returned, preferred_element_type=jnp.float32)
        ).astype(out.dtype)
    for d in range(experts):
        if d > 0:
            z_out[d].wait_send()
        y_out[d].wait_send()
        c_out[d].wait_send()
        f_out[d].wait_send()
        for j in range(n_down):
            c_back(d, j).wait_send()
            y_back(d, j).wait_send()
            if d > 0:
                z_back(d, j).wait_send()


def route(tokens, expert_ids, w_router, plane):
    experts = w_router.shape[1]
    count = tokens.shape[0]
    logits = jnp.dot(tokens, w_router, preferred_element_type=jnp.float32)
    labels = lax.axis_index("ep") // plane ^ jnp.arange(experts, dtype=jnp.int32)
    natural = jnp.arange(experts, dtype=jnp.int32)
    onehot = expert_ids[:, :, None] == natural[None, None, :]
    picked = jnp.sum(jnp.where(onehot, logits[:, None, :], jnp.float32(0.0)), axis=2)
    gates = 1.0 / (1.0 + jnp.exp(picked[:, ::-1] - picked))
    hit = expert_ids[:, :, None] == labels[None, None, :]
    any_hit = jnp.any(hit, axis=1)
    earlier = jnp.tri(count, count, -1, dtype=jnp.bfloat16)
    position = jnp.dot(
        earlier, any_hit.astype(jnp.bfloat16), preferred_element_type=jnp.float32
    ).astype(jnp.int32)
    gate_of = jnp.sum(jnp.where(hit, gates[:, :, None], 0.0), axis=1)
    slots = jnp.arange(CAP, dtype=jnp.int32)
    chosen = any_hit[:, :, None] & (position[:, :, None] == slots[None, None, :])
    chosen = chosen.reshape(count, experts * CAP)
    combine = jnp.where(
        chosen, jnp.repeat(gate_of, CAP, axis=1), jnp.float32(0.0)
    )
    packed = lax.dot_general(
        chosen.astype(jnp.bfloat16),
        tokens,
        (((0,), (0,)), ((), ())),
        preferred_element_type=jnp.float32,
    ).astype(jnp.bfloat16)
    comb_hi = combine.astype(jnp.bfloat16)
    comb_lo = (combine - comb_hi.astype(jnp.float32)).astype(jnp.bfloat16)
    return packed.reshape(experts, CAP, tokens.shape[1]), comb_hi, comb_lo


def on_device(
    tokens,
    expert_ids,
    w_router,
    w_gate,
    w_up,
    w_down,
    queries,
    key_cache,
    cached_value_rows,
    lengths,
):
    experts = w_router.shape[1]
    plane = lax.axis_size("ep") // experts
    count, features = tokens.shape
    width = w_gate.shape[1]
    packed, comb_hi, comb_lo = route(tokens, expert_ids, w_router, plane)
    requests, positions, kv_heads, head_dim = key_cache.shape
    flat = (requests, positions * kv_heads, head_dim)
    bf16 = jnp.bfloat16
    vmem = pl.BlockSpec(memory_space=pltpu.VMEM)
    smem = pl.BlockSpec(memory_space=pltpu.SMEM)
    hbm = pl.BlockSpec(memory_space=pl.ANY)
    n_up = width // UP_TILE
    n_down = features // DOWN_TILE
    return pl.pallas_call(
        functools.partial(moe_kernel, plane, kv_heads),
        out_shape=(
            jax.ShapeDtypeStruct((count, features), bf16),
            jax.ShapeDtypeStruct(queries.shape, bf16),
        ),
        in_specs=[vmem, vmem, vmem, vmem, smem, hbm, hbm, hbm, hbm, hbm],
        out_specs=(vmem, vmem),
        scratch_shapes=[
            pltpu.VMEM((n_up, features, UP_TILE), bf16),
            pltpu.VMEM((n_up, features, UP_TILE), bf16),
            pltpu.VMEM((n_down, width, DOWN_TILE), bf16),
            pltpu.VMEM(flat, bf16),
            pltpu.VMEM(flat, bf16),
            pltpu.VMEM((experts, plane, CAP, features), bf16),
            pltpu.VMEM((n_up, plane * CAP, UP_TILE), bf16),
            pltpu.VMEM((experts, n_down, plane, CAP, DOWN_TILE), bf16),
            pltpu.VMEM((experts, n_down, 2, CAP, DOWN_TILE), bf16),
            pltpu.VMEM((experts, n_down, CAP, DOWN_TILE), bf16),
            pltpu.VMEM((experts, n_down, CAP, DOWN_TILE), bf16),
            pltpu.SemaphoreType.DMA((2, n_up)),
            pltpu.SemaphoreType.DMA((n_down,)),
            pltpu.SemaphoreType.DMA((2,)),
            pltpu.SemaphoreType.DMA,
            pltpu.SemaphoreType.DMA((7, experts * n_down)),
            pltpu.SemaphoreType.DMA((7, experts * n_down)),
        ],
        compiler_params=pltpu.CompilerParams(
            collective_id=0, has_side_effects=True, vmem_limit_bytes=VMEM_LIMIT
        ),
    )(
        packed,
        comb_hi,
        comb_lo,
        queries,
        lengths,
        w_gate,
        w_up,
        w_down,
        key_cache.reshape(flat),
        cached_value_rows.reshape(flat),
    )


def solution(mesh):
    in_specs = (
        P(("group", "ep"), None),
        P(("group", "ep"), None),
        P(),
        P(None, "ep"),
        P(None, "ep"),
        P("ep", None),
        P(("group", "ep"), None, None),
        P(("group", "ep"), None, None, None),
        P(("group", "ep"), None, None, None),
        P(("group", "ep")),
    )
    out_specs = (P(("group", "ep"), None), P(("group", "ep"), None, None))
    return jax.shard_map(
        on_device, mesh=mesh, in_specs=in_specs, out_specs=out_specs, check_vma=False
    )
```

profile of v0, /device:TPU:0, one launch (start us, length us, event | category | flops | bytes accessed | tf_op | source)
XLA Modules:
  0.0 99.3 jit_solution(14700146765382385501)
XLA Ops:
  0.6 0.0 copy-start
  0.7 0.8 compare_reduce_fusion
  1.5 0.2 convolution_convert_fusion.1
  1.7 0.0 copy-done
  1.7 0.9 fusion.2
  2.6 0.7 select_reduce_fusion
  3.4 0.8 fusion.1
  4.2 0.1 eq.50
  4.3 0.1 copy.21
  4.4 0.1 copy.22
  4.5 0.1 copy.20
  4.6 0.6 subtract_convert_fusion
  5.2 0.6 select_convert_fusion.comb_hi
  5.8 1.5 %convolution_convert_fusion = bf16[192,3072]{1,0:T(8,128)(2,1)} fusion(pred[64,192]{1,0:T(32,128)(4,1)S(1)} %get-tuple-element.3, bf16[64,3072]{1,0:T(8,128)(2,1)S(1)} %copy-done), kind=kOutput, calls=%fused_computation | convolution fusion | flops 76087296 | bytes 1585152 | tf_op jit(solution)/shard_map/dot_general | solution.py:295
  7.3 88.8 %shard_map.113 = (bf16[64,3072]{1,0:T(8,128)(2,1)}, bf16[8,24,128]{2,1,0:T(8,128)(2,1)}) custom-call(bf16[4,48,3072]{2,1,0:T(8,128)(2,1)} %bitcast.11, bf16[64,192]{1,0:T(8,128)(2,1)} %select_convert_fusion.comb_hi, bf16[64,192]{1,0:T(8,128)(2,1)} %get-tuple-element.2.comb_lo, bf16[8,24,128]{2,1,0:T(8,128)(2,1)} %queries.1, s32[8]{0:T(128)} %lengths.1, ...), custom_call_target="tpu_custom_call" | custom-call | tf_op jit(solution)/shard_map/pallas_call | solution.py:331
  96.1 1.8 %copy.29 = bf16[64,3072]{1,0:T(8,128)(2,1)} copy(bf16[64,3072]{1,0:T(8,128)(2,1)} %get-tuple-element.6) | data formatting | bytes 786432
  97.9 1.4 %copy.30 = bf16[8,24,128]{2,1,0:T(8,128)(2,1)} copy(bf16[8,24,128]{2,1,0:T(8,128)(2,1)} %get-tuple-element.7) | data formatting | bytes 98304
  (8 shorter events, 0.1 us)
Async XLA Ops:
  0.6 1.1 %copy-start = (bf16[64,3072]{1,0:T(8,128)(2,1)S(1)}, bf16[64,3072]{1,0:T(8,128)(2,1)}, u32[]{:S(2)}) copy-start(bf16[64,3072]{1,0:T(8,128)(2,1)} %param.10) | copy-start | bytes 1179652
where the time goes:
time: 99.7 us; the launch traced here: 99.3 us
  Pallas kernels  88.8 us (89%)
  local copies, waits for them, and re-layouts  3.59 us (4%)
  other arithmetic  3.57 us (4%)
  matrix products  2.66 us (3%)
    pallas_call x1, Pallas kernels, on_device(): pl.pallas_call(functools.partial(moe_kernel, plane, kv_heads), out_shape=...  88.8 us
    unnamed x4, local copies, waits for them, and re-layouts  3.2 us

commit v1 on v0

v1 whole, which is shorter than its diff:
```python
import functools

import jax
import jax.numpy as jnp
from jax import lax
from jax.experimental import pallas as pl
from jax.experimental.pallas import tpu as pltpu
from jax.sharding import PartitionSpec as P

CAP = 48
UP_TILE = 512
DOWN_TILE = 1024
CHUNK = 1024
VMEM_LIMIT = 66_000_000
MESH = pl.DeviceIdType.MESH


def flip(index, mask):
    result = index
    bit = 1
    while bit <= mask:
        if mask & bit:
            result = result + bit - 2 * bit * ((index // bit) % 2)
        bit *= 2
    return result


def moe_kernel(
    plane,
    kv_heads,
    tokens,
    ids,
    router,
    queries,
    lengths,
    wg_hbm,
    wu_hbm,
    wd_hbm,
    k_hbm,
    v_hbm,
    out,
    att_out,
    wg,
    wu,
    wd,
    keys,
    values,
    pos,
    gate,
    comb,
    line,
    line_pos,
    outbox,
    arrived,
    hidden,
    partial,
    got_core,
    got_y,
    got_z,
    w_sems,
    d_sems,
    kv_sems,
    send_sems,
    recv_sems,
):
    me = lax.axis_index("ep")
    experts = router.shape[0]
    count, features = tokens.shape
    z = me // plane
    mid = (z % (experts - 1) + 1) // 2
    core_peer = flip(me, 1)
    y_peer = flip(me, 2)
    z_peers = [flip(me, plane * d) for d in range(experts)]
    xors = [0, 2 + mid, 3 - mid, 1]
    homes = [
        me,
        z_peers[2] + mid * (z_peers[3] - z_peers[2]),
        z_peers[3] + mid * (z_peers[2] - z_peers[3]),
        z_peers[1],
    ]
    n_up = wg.shape[0]
    n_down = wd.shape[0]
    up_tile = wg.shape[2]
    down_tile = wd.shape[2]

    def on_end(body):
        pl.when(mid == 0)(body)

    def on_mid(body):
        pl.when(mid == 1)(body)

    def kv_copy(i):
        src, dst = ((k_hbm, keys), (v_hbm, values))[i]
        return pltpu.make_async_copy(src, dst, kv_sems.at[i])

    def up_copy(i, j):
        src, dst = ((wg_hbm, wg), (wu_hbm, wu))[i]
        cols = pl.ds(pl.multiple_of(j * up_tile, up_tile), up_tile)
        return pltpu.make_async_copy(src.at[:, cols], dst.at[j], w_sems.at[i, j])

    def down_copy(j):
        cols = pl.ds(pl.multiple_of(j * down_tile, down_tile), down_tile)
        return pltpu.make_async_copy(wd_hbm.at[:, cols], wd.at[j], d_sems.at[j])

    barrier = pltpu.get_barrier_semaphore()
    peers = [core_peer, y_peer] + z_peers[1:]
    for peer in peers:
        pl.semaphore_signal(barrier, inc=1, device_id={"ep": peer}, device_id_type=MESH)
    kv_copy(0).start()
    kv_copy(1).start()
    up_copy(0, 0).start()
    up_copy(1, 0).start()

    row = lax.broadcasted_iota(jnp.int32, (8, count), 0)
    label = jnp.full((8, count), -1, jnp.int32)
    for d in range(experts):
        label = jnp.where(row == d, flip(z, d), label)
    first_hit = ids[0:1, :] == label
    second_hit = ids[1:2, :] == label
    hit = first_hit | second_hit
    before = (
        lax.broadcasted_iota(jnp.int32, (count, count), 0)
        < lax.broadcasted_iota(jnp.int32, (count, count), 1)
    )
    position = jnp.dot(
        hit.astype(jnp.float32).astype(jnp.bfloat16),
        before.astype(jnp.float32).astype(jnp.bfloat16),
        preferred_element_type=jnp.float32,
    )
    pos[...] = jnp.full(pos.shape, -1.0, jnp.float32)
    pos[:, 0:count] = jnp.where(hit, position, -1.0)
    pl.semaphore_wait(barrier, len(peers))
    for j in range(1, n_up):
        up_copy(0, j).start()
        up_copy(1, j).start()

    def remote(kind, index, src, dst, peer):
        return pltpu.make_async_remote_copy(
            src_ref=src,
            dst_ref=dst,
            send_sem=send_sems.at[kind, index],
            recv_sem=recv_sems.at[kind, index],
            device_id={"ep": peer},
            device_id_type=MESH,
        )

    chunks = features // CHUNK

    def span(k):
        return pl.ds(k * CHUNK, CHUNK)

    def dense(d, k, src, peer):
        return remote(
            0, d * chunks + k, src.at[:, span(k)], line.at[d - 1, :, span(k)], peer
        )

    def slots(d, src, peer):
        return remote(1, d, src, line_pos.at[d - 1], peer)

    def end_dense(k):
        return dense(1, k, tokens, z_peers[1])

    def mid_dense(k):
        return dense(3, k, tokens, z_peers[3])

    def fwd_dense(k):
        return dense(2, k, line.at[0], z_peers[3])

    end_slots = slots(1, pos, z_peers[1])
    mid_slots = slots(3, pos, z_peers[3])
    fwd_slots = slots(2, line_pos.at[0], z_peers[3])

    def box(p, k):
        return remote(
            2,
            p * chunks + k,
            outbox.at[p - 1, :, span(k)],
            arrived.at[p, 0, :, span(k)],
            z_peers[1],
        )

    def within(kind, p, k, source, target, peer):
        return remote(
            kind,
            p * chunks + k,
            arrived.at[p, source, :, span(k)],
            arrived.at[p, target, :, span(k)],
            peer,
        )

    def y_out(p, k):
        return within(3, p, k, 0, 1, y_peer)

    def c_out(p, k):
        return within(4, p, k, 0, 2, core_peer)

    def f_out(p, k):
        return within(5, p, k, 1, 3, core_peer)

    def c_back(p, j):
        return remote(
            6, p * n_down + j, partial.at[p, j, pl.ds(2, 2)], got_core.at[p, j], core_peer
        )

    def y_back(p, j):
        return remote(7, p * n_down + j, partial.at[p, j, 1], got_y.at[p, j], y_peer)

    def z_back(p, d, j, peer):
        return remote(8, d * n_down + j, partial.at[p, j, 0], got_z.at[d, j], peer)

    def pack(dst, slot, src, k):
        cap = dst.shape[0]
        wanted = lax.broadcasted_iota(jnp.int32, (cap, count), 0).astype(jnp.float32)
        pick = jnp.where(wanted == slot[:, 0:count], 1.0, 0.0).astype(jnp.bfloat16)
        dst[:, span(k)] = jnp.dot(
            pick, src[:, span(k)], preferred_element_type=jnp.float32
        ).astype(jnp.bfloat16)

    def spread(p, k):
        y_out(p, k).start()
        c_out(p, k).start()

    def forward(p, k):
        y_out(p, k).wait_recv()
        f_out(p, k).start()

    def settle(p):
        for k in range(chunks):
            c_out(p, k).wait_recv()
            f_out(p, k).wait_recv()

    @on_end
    def _():
        end_slots.start()
        for k in range(chunks):
            end_dense(k).start()

    @on_mid
    def _():
        mid_slots.start()
        for k in range(chunks):
            mid_dense(k).start()

    for k in range(chunks):
        pack(arrived.at[0, 0], pos[0:1, :], tokens, k)
        spread(0, k)

    @on_mid
    def _():
        for k in range(chunks):
            pack(outbox.at[2], pos[1:2, :], tokens, k)
            box(3, k).start()

    logits = lax.dot_general(
        router[...], tokens[...], (((1,), (1,)), ((), ())), preferred_element_type=jnp.float32
    )
    natural = lax.broadcasted_iota(jnp.int32, (experts, count), 0)
    first = jnp.sum(jnp.where(ids[0:1, :] == natural, logits, 0.0), axis=0, keepdims=True)
    second = jnp.sum(jnp.where(ids[1:2, :] == natural, logits, 0.0), axis=0, keepdims=True)
    first_gate = 1.0 / (1.0 + jnp.exp(second - first))
    second_gate = 1.0 / (1.0 + jnp.exp(first - second))
    gate[...] = jnp.zeros(gate.shape, jnp.float32)
    gate[:, 0:count] = jnp.where(first_hit, first_gate, 0.0) + jnp.where(
        second_hit, second_gate, 0.0
    )
    lanes = pos.shape[1]
    columns = jnp.concatenate(
        [pos[...], gate[...], jnp.zeros((lanes - 16, lanes), jnp.float32)], axis=0
    ).T
    width = experts * CAP
    slot = lax.broadcasted_iota(jnp.int32, (count, width), 1)
    weight = jnp.zeros((count, width), jnp.float32)
    for d in range(experts):
        inside = slot.astype(jnp.float32) == columns[0:count, d : d + 1] + float(d * CAP)
        inside = inside & (columns[0:count, d : d + 1] >= 0.0)
        weight = jnp.where(inside, columns[0:count, 8 + d : 9 + d], weight)
    high = weight.astype(jnp.bfloat16)
    comb[0] = high
    comb[1] = (weight - high.astype(jnp.float32)).astype(jnp.bfloat16)

    kv_copy(0).wait()
    kv_copy(1).wait()
    heads, head_dim = queries.shape[1], queries.shape[2]
    rows = keys.shape[1]

    def attend(r, carry):
        scores = lax.dot_general(
            queries[r], keys[r], (((1,), (1,)), ((), ())), preferred_element_type=jnp.float32
        ) * head_dim ** (-0.5)
        col = lax.broadcasted_iota(jnp.int32, (heads, rows), 1)
        head = lax.broadcasted_iota(jnp.int32, (heads, rows), 0)
        keep = (col % kv_heads == head // (heads // kv_heads)) & (
            col // kv_heads < lengths[r]
        )
        scores = jnp.where(keep, scores, -jnp.inf)
        top = jnp.max(scores, axis=1, keepdims=True)
        expo = jnp.exp(scores - top)
        weights = (expo / jnp.sum(expo, axis=1, keepdims=True)).astype(jnp.bfloat16)
        mixed = jnp.dot(weights, values[r], preferred_element_type=jnp.float32)
        att_out[r] = mixed.astype(att_out.dtype)
        return carry

    lax.fori_loop(0, queries.shape[0], attend, 0)
    for j in range(n_down):
        down_copy(j).start()

    def attend_to(services, j):
        for at, want, action in services:
            pl.when((j == at) if want is None else (j == at) & (mid == want))(action)

    def gate_up(p, wait, services=()):
        block = arrived.at[p]
        m = block.shape[0] * block.shape[1]

        def step(j, carry):
            if wait:
                up_copy(0, j).wait()
                up_copy(1, j).wait()
            x = block[...].reshape(m, features)
            g = jnp.dot(x, wg[j], preferred_element_type=jnp.float32)
            u = jnp.dot(x, wu[j], preferred_element_type=jnp.float32)
            hidden[j] = (g / (1.0 + jnp.exp(-g)) * u).astype(jnp.bfloat16)
            attend_to(services, j)
            return carry

        lax.fori_loop(0, n_up, step, 0)

    def down(p, wait, services=()):
        def step(j, carry):
            if wait:
                down_copy(j).wait()
            h = jnp.concatenate([hidden[i] for i in range(n_up)], axis=1)
            o = jnp.dot(h, wd[j], preferred_element_type=jnp.float32)
            partial[p, j] = o.astype(jnp.bfloat16).reshape(partial.shape[2:])
            c_back(p, j).start()
            attend_to(services, j)
            return carry

        lax.fori_loop(0, n_down, step, 0)

    def sum_core(p, j):
        def action():
            c_back(p, j).wait_recv()
            for s in (1, 0):
                partial[p, j, s] = (
                    partial[p, j, s].astype(jnp.float32) + got_core[p, j, s].astype(jnp.float32)
                ).astype(jnp.bfloat16)
            y_back(p, j).start()

        return action

    def sum_y(p, j):
        def action():
            y_back(p, j).wait_recv()
            total = partial[p, j, 0].astype(jnp.float32) + got_y[p, j].astype(jnp.float32)
            if p == 0:
                got_z[0, j] = total.astype(jnp.bfloat16)
            else:
                partial[p, j, 0] = total.astype(jnp.bfloat16)
                z_back(p, xors[p], j, homes[p]).start()

        return action

    def take(p, k):
        def action():
            box(p, k).wait_recv()
            spread(p, k)

        return action

    def near(k):
        def action():
            end_dense(k).wait_recv()
            fwd_dense(k).start()
            mid_dense(k).wait_recv()
            pack(arrived.at[1, 0], line_pos[2, 3:4, :], line.at[2], k)
            spread(1, k)
            pack(outbox.at[0], line_pos[2, 2:3, :], line.at[2], k)
            box(1, k).start()
            pack(arrived.at[3, 0], line_pos[0, 1:2, :], line.at[0], k)
            spread(3, k)

        return action

    def far(k):
        def action():
            if k == 0:
                fwd_slots.wait_recv()
            fwd_dense(k).wait_recv()
            pack(outbox.at[1], line_pos[1, 3:4, :], line.at[1], k)
            box(2, k).start()
            pack(arrived.at[2, 0], line_pos[1, 2:3, :], line.at[1], k)
            spread(2, k)

        return action

    def forwards(p):
        for k in range(chunks):
            forward(p, k)

    @on_end
    def _():
        for k in range(chunks):
            forward(0, k)
            take(3, k)()

    @on_mid
    def _():
        end_slots.wait_recv()
        fwd_slots.start()
        mid_slots.wait_recv()
        for k in range(chunks - 1):
            forward(0, k)
            near(k)()
        forward(0, chunks - 1)

    settle(0)
    gate_up(
        0,
        True,
        [
            (1, 1, near(chunks - 1)),
            (2, 0, take(1, 0)),
            (3, 0, take(1, 1)),
            (3, 1, far(0)),
        ],
    )
    down(0, True, [(1, 1, far(1)), (1, 0, take(1, 2))])
    forwards(1)
    settle(1)
    gate_up(
        1,
        False,
        [(0, 1, far(2)), (0, 0, take(2, 0)), (1, 0, take(2, 1)), (3, 0, take(2, 2))],
    )
    forwards(3)
    down(1, False, [(1, None, sum_core(1, 0)), (2, None, sum_core(1, 1))])
    forwards(2)
    sum_core(1, 2)()
    sum_core(0, 0)()
    settle(2)
    gate_up(2, False, [(3, None, sum_y(1, 0))])
    down(
        2,
        False,
        [
            (1, None, sum_core(2, 0)),
            (1, None, sum_y(1, 1)),
            (2, None, sum_core(2, 1)),
            (2, None, sum_y(1, 2)),
        ],
    )
    sum_core(2, 2)()
    sum_core(0, 1)()
    settle(3)
    gate_up(3, False, [(3, None, sum_y(2, 0))])
    down(
        3,
        False,
        [
            (1, None, sum_core(3, 0)),
            (1, None, sum_y(2, 1)),
            (2, None, sum_core(3, 1)),
            (2, None, sum_y(2, 2)),
        ],
    )
    sum_core(3, 2)()
    sum_core(0, 2)()
    for j in range(n_down):
        sum_y(3, j)()
    for j in range(n_down):
        sum_y(0, j)()
    for j in range(n_down):
        for d in range(1, experts):
            z_back(d, d, j, z_peers[d]).wait_recv()
        returned = got_z[:, j].reshape(experts * got_z.shape[2], down_tile)
        out[:, j * down_tile : (j + 1) * down_tile] = (
            jnp.dot(comb[0], returned, preferred_element_type=jnp.float32)
            + jnp.dot(comb[1], returned, preferred_element_type=jnp.float32)
        ).astype(out.dtype)

    @on_end
    def _():
        end_slots.wait_send()
        for k in range(chunks):
            end_dense(k).wait_send()

    @on_mid
    def _():
        mid_slots.wait_send()
        fwd_slots.wait_send()
        for k in range(chunks):
            mid_dense(k).wait_send()
            fwd_dense(k).wait_send()
            for p in range(1, experts):
                box(p, k).wait_send()

    for p in range(experts):
        for k in range(chunks):
            y_out(p, k).wait_send()
            c_out(p, k).wait_send()
            f_out(p, k).wait_send()
        for j in range(n_down):
            c_back(p, j).wait_send()
            y_back(p, j).wait_send()
            if p > 0:
                z_back(p, p, j, z_peers[p]).wait_send()


def fused(
    plane,
    tokens,
    expert_ids,
    w_router,
    w_gate,
    w_up,
    w_down,
    queries,
    key_cache,
    cached_value_rows,
    lengths,
):
    experts = w_router.shape[1]
    count, features = tokens.shape
    width = w_gate.shape[1]
    requests, positions, kv_heads, head_dim = key_cache.shape
    flat = (requests, positions * kv_heads, head_dim)
    bf16 = jnp.bfloat16
    f32 = jnp.float32
    lanes = 128
    vmem = pl.BlockSpec(memory_space=pltpu.VMEM)
    smem = pl.BlockSpec(memory_space=pltpu.SMEM)
    hbm = pl.BlockSpec(memory_space=pl.ANY)
    n_up = width // UP_TILE
    n_down = features // DOWN_TILE
    return pl.pallas_call(
        functools.partial(moe_kernel, plane, kv_heads),
        out_shape=(
            jax.ShapeDtypeStruct((count, features), bf16),
            jax.ShapeDtypeStruct(queries.shape, bf16),
        ),
        in_specs=[vmem, vmem, vmem, vmem, smem, hbm, hbm, hbm, hbm, hbm],
        out_specs=(vmem, vmem),
        scratch_shapes=[
            pltpu.VMEM((n_up, features, UP_TILE), bf16),
            pltpu.VMEM((n_up, features, UP_TILE), bf16),
            pltpu.VMEM((n_down, width, DOWN_TILE), bf16),
            pltpu.VMEM(flat, bf16),
            pltpu.VMEM(flat, bf16),
            pltpu.VMEM((8, lanes), f32),
            pltpu.VMEM((8, lanes), f32),
            pltpu.VMEM((2, count, experts * CAP), bf16),
            pltpu.VMEM((experts - 1, count, features), bf16),
            pltpu.VMEM((experts - 1, 8, lanes), f32),
            pltpu.VMEM((experts - 1, CAP, features), bf16),
            pltpu.VMEM((experts, plane, CAP, features), bf16),
            pltpu.VMEM((n_up, plane * CAP, UP_TILE), bf16),
            pltpu.VMEM((experts, n_down, plane, CAP, DOWN_TILE), bf16),
            pltpu.VMEM((experts, n_down, 2, CAP, DOWN_TILE), bf16),
            pltpu.VMEM((experts, n_down, CAP, DOWN_TILE), bf16),
            pltpu.VMEM((experts, n_down, CAP, DOWN_TILE), bf16),
            pltpu.SemaphoreType.DMA((2, n_up)),
            pltpu.SemaphoreType.DMA((n_down,)),
            pltpu.SemaphoreType.DMA((2,)),
            pltpu.SemaphoreType.DMA((9, experts * n_down)),
            pltpu.SemaphoreType.DMA((9, experts * n_down)),
        ],
        compiler_params=pltpu.CompilerParams(
            collective_id=0, has_side_effects=True, vmem_limit_bytes=VMEM_LIMIT
        ),
    )(
        tokens,
        expert_ids.T,
        w_router.T,
        queries,
        lengths,
        w_gate,
        w_up,
        w_down,
        key_cache.reshape(flat),
        cached_value_rows.reshape(flat),
    )


def general(
    share,
    tokens,
    expert_ids,
    w_router,
    w_gate,
    w_up,
    w_down,
    queries,
    key_cache,
    cached_value_rows,
    lengths,
):
    f32 = jnp.float32
    experts = w_router.shape[1]
    logits = jnp.dot(tokens, w_router, preferred_element_type=f32)
    onehot = expert_ids[:, :, None] == jnp.arange(experts, dtype=jnp.int32)[None, None, :]
    picked = jnp.sum(jnp.where(onehot, logits[:, None, :], 0.0), axis=2)
    gates = 1.0 / (1.0 + jnp.exp(picked[:, ::-1] - picked))
    gate_of = jnp.sum(jnp.where(onehot, gates[:, :, None], 0.0), axis=1)
    everyone = lax.all_gather(tokens, "ep", tiled=True)
    gate_of = lax.all_gather(gate_of, "ep", tiled=True)
    mine = jnp.arange(experts, dtype=jnp.int32) == lax.axis_index("ep") // share
    weight = jnp.sum(jnp.where(mine[None, :], gate_of, 0.0), axis=1, keepdims=True)
    g = jnp.dot(everyone, w_gate, preferred_element_type=f32)
    u = jnp.dot(everyone, w_up, preferred_element_type=f32)
    hidden = (g / (1.0 + jnp.exp(-g)) * u).astype(jnp.bfloat16)
    part = jnp.dot(hidden, w_down, preferred_element_type=f32) * weight
    moe_out = lax.psum_scatter(part, "ep", scatter_dimension=0, tiled=True).astype(jnp.bfloat16)
    requests, heads, head_dim = queries.shape
    positions, kv_heads = key_cache.shape[1:3]
    grouped = queries.reshape(requests, kv_heads, heads // kv_heads, head_dim)
    scores = jnp.einsum(
        "bkgd,blkd->bkgl", grouped, key_cache, preferred_element_type=f32
    ) * head_dim ** (-0.5)
    visible = jnp.arange(positions, dtype=jnp.int32)[None, :] < lengths[:, None]
    weights = jax.nn.softmax(jnp.where(visible[:, None, None, :], scores, -jnp.inf), axis=3)
    mixed = jnp.einsum(
        "bkgl,blkd->bkgd",
        weights.astype(jnp.bfloat16),
        cached_value_rows,
        preferred_element_type=f32,
    )
    return moe_out, mixed.reshape(queries.shape).astype(jnp.bfloat16)


def on_device(*args):
    experts = args[2].shape[1]
    share = lax.axis_size("ep") // experts
    body = fused if experts == 4 and share == 4 else general
    return body(share, *args)


def solution(mesh):
    in_specs = (
        P(("group", "ep"), None),
        P(("group", "ep"), None),
        P(),
        P(None, "ep"),
        P(None, "ep"),
        P("ep", None),
        P(("group", "ep"), None, None),
        P(("group", "ep"), None, None, None),
        P(("group", "ep"), None, None, None),
        P(("group", "ep")),
    )
    out_specs = (P(("group", "ep"), None), P(("group", "ep"), None, None))
    return jax.shard_map(
        on_device, mesh=mesh, in_specs=in_specs, out_specs=out_specs, check_vma=False
    )
```

time: 99.7 us -> 84.6 us (0.85)
  Pallas kernels: 88.8 us -> 80.5 us
  other arithmetic: 3.57 us -> 0 us
  matrix products: 2.66 us -> 0 us
    pallas_call x1, Pallas kernels: 88.8 us -> 80.5 us  [fused(): pl.pallas_call(functools.partial(moe_kernel, plane, kv_heads), out_shape=...]
    dot_general x3 -> x0, matrix products: 2.66 us -> none  [the longest x1 1.52 us: route(): lax.dot_general(chosen.astype(jnp.bfloat16), tokens, (((0,), (0,)), ((),...]
    reduce_sum x2 -> x0, other arithmetic: 1.48 us -> none  [the longest x1 0.77 us: route(): gate_of = jnp.sum(jnp.where(hit, gates[:, :, None], 0.0), axis=1)]
    convert_element_type x2 -> x0, other arithmetic: 1.26 us -> none  [the longest x1 0.64 us: route(): comb_lo = (combine - comb_hi.astype(jnp.float32)).astype(jnp.bfloat16)]
    unnamed x4 -> x2, local copies, waits for them, and re-layouts: 3.2 us -> 3.19 us
where the time goes in v1:
time: 84.6 us; the launch traced here: 84.4 us
  Pallas kernels  80.5 us (95%)
  local copies, waits for them, and re-layouts  3.19 us (4%)
    pallas_call x1, Pallas kernels, fused(): pl.pallas_call(functools.partial(moe_kernel, plane, kv_heads), out_shape=...  80.5 us
    unnamed x2, local copies, waits for them, and re-layouts  3.19 us

profile of v1, /device:TPU:0, one launch (start us, length us, event | category | flops | bytes accessed | tf_op | source)
XLA Modules:
  0.0 84.4 jit_solution(2331206695351954916)
XLA Ops:
  0.6 80.5 %shard_map.113 = (bf16[64,3072]{1,0:T(8,128)(2,1)}, bf16[8,24,128]{2,1,0:T(8,128)(2,1)}) custom-call(bf16[64,3072]{1,0:T(8,128)(2,1)} %tokens.1, s32[2,64]{1,0:T(2,128)} %bitcast.7, bf16[4,3072]{1,0:T(4,128)(2,1)} %bitcast.6, bf16[8,24,128]{2,1,0:T(8,128)(2,1)} %queries.1, s32[8]{0:T(128)} %lengths.1, bf16[3072,2048]{1,0:T(8,128)(2,1)} %wg_hbm.1, ...), custom_call_target="tpu_custom_call" | custom-call | tf_op jit(solution)/shard_map/pallas_call | solution.py:536
  81.2 1.8 %copy.14 = bf16[64,3072]{1,0:T(8,128)(2,1)} copy(bf16[64,3072]{1,0:T(8,128)(2,1)} %get-tuple-element.4) | data formatting | bytes 786432
  83.0 1.4 %copy.15 = bf16[8,24,128]{2,1,0:T(8,128)(2,1)} copy(bf16[8,24,128]{2,1,0:T(8,128)(2,1)} %get-tuple-element.5) | data formatting | bytes 98304

commit v2 on v1

--- a/solution.py
+++ b/solution.py
@@ -394,6 +394,9 @@
 
         return action
 
+    def pass_on(p, k):
+        return lambda: forward(p, k)
+
     def forwards(p):
         for k in range(chunks):
             forward(p, k)
@@ -423,10 +426,19 @@
             (2, 0, take(1, 0)),
             (3, 0, take(1, 1)),
             (3, 1, far(0)),
+            (3, None, pass_on(1, 0)),
         ],
     )
-    down(0, True, [(1, 1, far(1)), (1, 0, take(1, 2))])
-    forwards(1)
+    down(
+        0,
+        True,
+        [
+            (0, 0, take(1, 2)),
+            (0, None, pass_on(1, 1)),
+            (1, 1, far(1)),
+            (1, None, pass_on(1, 2)),
+        ],
+    )
     settle(1)
     gate_up(
         1,
@@ -434,12 +446,23 @@
         [(0, 1, far(2)), (0, 0, take(2, 0)), (1, 0, take(2, 1)), (3, 0, take(2, 2))],
     )
     forwards(3)
-    down(1, False, [(1, None, sum_core(1, 0)), (2, None, sum_core(1, 1))])
-    forwards(2)
-    sum_core(1, 2)()
-    sum_core(0, 0)()
+    down(
+        1,
+        False,
+        [
+            (0, None, pass_on(2, 0)),
+            (1, None, sum_core(1, 0)),
+            (1, None, pass_on(2, 1)),
+            (2, None, sum_core(1, 1)),
+            (2, None, pass_on(2, 2)),
+        ],
+    )
     settle(2)
-    gate_up(2, False, [(3, None, sum_y(1, 0))])
+    gate_up(
+        2,
+        False,
+        [(0, None, sum_core(1, 2)), (0, None, sum_core(0, 0)), (3, None, sum_y(1, 0))],
+    )
     down(
         2,
         False,
@@ -450,21 +473,24 @@
             (2, None, sum_y(1, 2)),
         ],
     )
-    sum_core(2, 2)()
-    sum_core(0, 1)()
     settle(3)
-    gate_up(3, False, [(3, None, sum_y(2, 0))])
+    gate_up(
+        3,
+        False,
+        [(0, None, sum_core(2, 2)), (0, None, sum_core(0, 1))],
+    )
     down(
         3,
         False,
         [
             (1, None, sum_core(3, 0)),
-            (1, None, sum_y(2, 1)),
+            (1, None, sum_y(2, 0)),
             (2, None, sum_core(3, 1)),
-            (2, None, sum_y(2, 2)),
+            (2, None, sum_y(2, 1)),
         ],
     )
     sum_core(3, 2)()
+    sum_y(2, 2)()
     sum_core(0, 2)()
     for j in range(n_down):
         sum_y(3, j)()

time: 84.6 us -> 84 us (level)
  no operation moved by 1% of the time
where the time goes in v2:
time: 84 us; the launch traced here: 83.8 us
  Pallas kernels  80 us (95%)
  local copies, waits for them, and re-layouts  3.19 us (4%)
    pallas_call x1, Pallas kernels, fused(): pl.pallas_call(functools.partial(moe_kernel, plane, kv_heads), out_shape=...  80 us
    unnamed x2, local copies, waits for them, and re-layouts  3.19 us

profile of v2, /device:TPU:0, one launch (start us, length us, event | category | flops | bytes accessed | tf_op | source)
XLA Modules:
  0.0 83.8 jit_solution(36963190509905983)
XLA Ops:
  0.6 80.0 %shard_map.113 = (bf16[64,3072]{1,0:T(8,128)(2,1)}, bf16[8,24,128]{2,1,0:T(8,128)(2,1)}) custom-call(bf16[64,3072]{1,0:T(8,128)(2,1)} %tokens.1, s32[2,64]{1,0:T(2,128)} %bitcast.7, bf16[4,3072]{1,0:T(4,128)(2,1)} %bitcast.6, bf16[8,24,128]{2,1,0:T(8,128)(2,1)} %queries.1, s32[8]{0:T(128)} %lengths.1, bf16[3072,2048]{1,0:T(8,128)(2,1)} %wg_hbm.1, ...), custom_call_target="tpu_custom_call" | custom-call | tf_op jit(solution)/shard_map/pallas_call | solution.py:562
  80.6 1.8 %copy.14 = bf16[64,3072]{1,0:T(8,128)(2,1)} copy(bf16[64,3072]{1,0:T(8,128)(2,1)} %get-tuple-element.4) | data formatting | bytes 786432
  82.4 1.4 %copy.15 = bf16[8,24,128]{2,1,0:T(8,128)(2,1)} copy(bf16[8,24,128]{2,1,0:T(8,128)(2,1)} %get-tuple-element.5) | data formatting | bytes 98304
